TPU v7x, 32 devices: a whole 2x2x4 slice. The times are simulated.
32 devices in a mesh: row: 8 (over y, x, core), col: 4 (over z).
Axes of the slice: x: 2, y: 2, z: 4, core: 2. Of those that a mesh axis runs over, the one named last changes fastest.
Arguments:
- schur: float32 [16384, 16384], P(None, ('row', 'col')), may hold values from -0.3 to 0.3
- basis: float32 [16384, 128], P('row'), may hold values from -1 to 1, as said below
- eigen: float32 [16384], P('row'), may hold values from -4 to -1
- schur_basis: bfloat16 [16384, 16384], P('col', 'row'), may hold values from -0.046875 to 0.046875
- rhs: bfloat16 [16384, 16384], P('col', 'row'), may hold values from -18 to 18, as said below
- inputs: bfloat16 [16384, 64], P('col'), may hold values from -6 to 6
Outputs:
- solution: float32 [16384, 128], P('row')
- feedback: float32 [64, 16384], P(None, 'col')
Inputs may be any that keep to these rules, and one draw needn't show every extreme that they name: `basis`: every block of 128 consecutive rows, starting at a multiple of 128, is an orthogonal 128 x 128 matrix. `rhs`: symmetric.
All inputs are finite; a program needn't handle non-finite values.
Results may differ from a plain program's by a relative error of at most 0.005.
Values may be sent and summed in bfloat16 or wider, within the bound.
A program may use at most 192 MiB of HBM per device.

v0:
```python
import jax
import jax.numpy as jnp
from jax import lax
from jax.sharding import PartitionSpec as P

TILE = 128
W_COLS = 128


HIGH = lax.Precision.HIGHEST


def spread(x, axis, root):
    mine = lax.axis_index(axis) == root
    return lax.psum(jnp.where(mine, x, jnp.zeros_like(x)), axis)


def tile_solve(right, basis_left, eig_left, basis_right, eig_right):
    rotated = jnp.dot(jnp.dot(basis_left.T, right, precision=HIGH), basis_right, precision=HIGH)
    scaled = rotated / (eig_left[:, None] + eig_right[None, :])
    return jnp.dot(jnp.dot(basis_left, scaled, precision=HIGH), basis_right.T, precision=HIGH)


def solve_rows(right, panel, basis_rows, eig_rows, corner_basis, corner_eig):
    count = right.shape[0] // TILE

    def step(index, solved):
        start = index * TILE
        column = lax.dynamic_slice_in_dim(panel, start, TILE, 1)
        earlier_sum = lax.dot_general(
            column,
            solved,
            (((0,), (0,)), ((), ())),
            precision=HIGH,
            preferred_element_type=jnp.float32,
        )
        local = lax.dynamic_slice_in_dim(right, start, TILE, 0) - earlier_sum
        bas = lax.dynamic_slice_in_dim(basis_rows, start, TILE, 0)
        eig = lax.dynamic_slice_in_dim(eig_rows, start, TILE, 0)
        pieces = [tile_solve(local, bas, eig, corner_basis, corner_eig)]
        return lax.dynamic_update_slice_in_dim(solved, jnp.concatenate(pieces, 1), start, 0)

    return lax.fori_loop(0, count, step, jnp.zeros(right.shape, jnp.float32))


def on_device(schur, basis, eigen, schur_basis, rhs, inputs):
    span = schur_basis.shape[1]
    chain = lax.axis_size("row")
    groups = lax.axis_size("col")
    ratio = chain // groups
    row_index = lax.axis_index("row")
    panel_rows = lax.dynamic_slice_in_dim(schur, row_index * span, span, 0)
    panel = lax.all_gather(panel_rows.astype(jnp.bfloat16), "col", axis=1, tiled=True).astype(
        panel_rows.dtype
    )
    corner, corner_basis, corner_eig = (
        spread(panel[:W_COLS, :W_COLS], "row", 0),
        spread(basis[:W_COLS], "row", 0),
        spread(eigen[:W_COLS], "row", 0),
    )
    window = spread(schur_basis[:, :W_COLS], "row", 0)
    offset = row_index % ratio * span
    mine = lax.dynamic_slice_in_dim(window, offset, span, 0)
    own_window = spread(mine, "col", row_index // ratio)
    partial_value = jnp.dot(rhs, own_window, preferred_element_type=jnp.float32)
    projected = lax.psum(partial_value, "row").astype(jnp.bfloat16)
    coords = lax.dot_general(
        schur_basis, projected, (((0,), (0,)), ((), ())), preferred_element_type=jnp.float32
    )
    share = lax.psum_scatter(coords, "col", scatter_dimension=0, tiled=True)

    def section(index, carry):
        residual, solution = carry
        gathered = lax.all_gather(residual, "col", axis=0, tiled=True)
        solved = solve_rows(gathered, panel, basis, eigen, corner_basis, corner_eig)
        solution = jnp.where(row_index == index, solved, solution)
        block = spread(solved, "row", index)
        weights = lax.dynamic_slice_in_dim(schur, index * span, span, 0)
        update = lax.dot_general(
            weights,
            block,
            (((0,), (0,)), ((), ())),
            precision=HIGH,
            preferred_element_type=jnp.float32,
        )
        residual = jnp.where(row_index > index, residual - update, residual)
        return (residual, solution)

    start_solution = jnp.zeros((span, W_COLS), jnp.float32)
    residual, solution = lax.fori_loop(0, chain, section, (-share, start_solution))
    mapped = lax.dot_general(
        inputs, schur_basis, (((0,), (0,)), ((), ())), preferred_element_type=jnp.float32
    )
    gain = lax.psum(jnp.dot(mapped, solution, precision=HIGH), ("row", "col"))
    feedback = jnp.dot(gain, window.astype(jnp.float32).T, precision=HIGH)
    return (solution, feedback)


def solution(mesh):
    placed = (
        P(None, ("row", "col")),
        P("row", None),
        P("row"),
        P("col", "row"),
        P("col", "row"),
        P("col", None),
    )
    return jax.shard_map(
        on_device,
        mesh=mesh,
        in_specs=placed,
        out_specs=(P("row", None), P(None, "col")),
        check_vma=False,
    )
```

profile of v0, /device:TPU:0, one launch (start us, length us, event | category | flops | bytes accessed | tf_op | source)
XLA Modules:
  0.0 2290.1 jit_solution(7209625041219928812)
XLA Ops:
  9.7 61.5 %all-reduce.7.cloned.1.call-done = bf16[4096,128]{1,0:T(8,128)(2,1)} async-done(((bf16[4096,128]{1,0:T(8,128)(2,1)}), bf16[4096,128]{1,0:T(8,128)(2,1)}) %all-reduce.7.cloned.1.call-update) | async-done | bytes 1048592 | tf_op jit(solution)/shard_map/psum | solution.py:15
  73.9 38.1 %all-reduce.9.cloned.1.call-done = bf16[2048,128]{1,0:T(8,128)(2,1)} async-done(((bf16[2048,128]{1,0:T(8,128)(2,1)}), bf16[2048,128]{1,0:T(8,128)(2,1)}) %all-reduce.9.cloned.1.call-update) | async-done | bytes 524304 | tf_op jit(solution)/shard_map/psum | solution.py:15
  112.0 11.7 convolution_bitcast_fusion
  123.7 57.6 %all-reduce.14 = (bf16[4096,128]{0,1:T(8,128)(2,1)}, f32[128]{0:T(128)S(1)}) all-reduce(f32[4096,128]{0,1:T(8,128)S(1)} %convolution_bitcast_fusion, f32[128]{0:T(128)S(1)} %broadcast_select_fusion.1), channel_id=1, replica_groups=mesh['row'=8,'col'=4] {'row'}, use_global_device_ids=true, to_apply=%region_2.3 | all-reduce | flops 524416 | bytes 3146752 | tf_op jit(solution)/shard_map/psum | solution.py:66
  217.9 148.5 %all-gather.3.cloned.1.call-done = bf16[2048,2048]{1,0:T(8,128)(2,1)} async-done(((bf16[2048,512]{1,0:T(8,128)(2,1)}), bf16[2048,2048]{1,0:T(8,128)(2,1)}) %all-gather.3.cloned.1.call-update) | async-done | bytes 8388624 | tf_op jit(solution)/shard_map/all_gather | solution.py:53
  377.6 43.7 %all-reduce.11.cloned.1.call-done = f32[128,128]{1,0:T(8,128)} async-done(((f32[128,128]{1,0:T(8,128)}), f32[128,128]{1,0:T(8,128)}) %all-reduce.11.cloned.1.call-update) | async-done | bytes 65552 | tf_op jit(solution)/shard_map/psum | solution.py:15
  421.2 1818.5 %while.43 = (s32[]{:T(128)}, f32[512,128]{1,0:T(8,128)S(1)}, f32[2048,128]{1,0:T(8,128)S(1)}, s32[]{:T(128)}, f32[16384,512]{1,0:T(8,128)}, /*index=5*/f32[2048,...) while((s32[]{:T(128)}, f32[512,128]{1,0:T(8,128)S(1)}, ...), condition=%wide.region_10.11_spmd.clone, body=%wide.region_6.10_spmd.clone.sunk | while | flops 2115158016 | bytes 26349272 | solution.py:90
  422.1 29.2 %all-gather.5.cloned.1.call-done = f32[2048,128]{1,0:T(8,128)} async-done(((f32[512,128]{1,0:T(8,128)}), f32[2048,128]{1,0:T(8,128)}) %all-gather.5.cloned.1.call-update) | async-done | bytes 1048592 | tf_op jit(solution)/shard_map/while/body/eval_jaxpr/all_gather | solution.py:74
  451.4 130.9 %while.44 = (s32[]{:T(128)}, f32[2048,128]{1,0:T(8,128)S(1)}, f32[2048,128]{1,0:T(8,128)}, f32[2048,128]{1,0:T(8,128)}, f32[2048,2048]{1,0:T(8,128)}, /*index=5*...) while((s32[]{:T(128)}, f32[2048,128]{1,0:T(8,128)S(1)}, ...), condition=%wide.region_8.8_spmd, body=%wide.region_7.7_spmd.sunk | while | flops 503365632 | bytes 3017907 | solution.py:43
  583.6 56.2 %all-reduce.13.cloned.1.call-done = f32[2048,128]{1,0:T(8,128)} async-done(((f32[2048,128]{1,0:T(8,128)}), f32[2048,128]{1,0:T(8,128)}) %all-reduce.13.cloned.1.call-update) | async-done | bytes 1048592 | tf_op jit(solution)/shard_map/while/body/eval_jaxpr/psum | solution.py:15
  649.5 29.4 %all-gather.5.cloned.1.call-done = f32[2048,128]{1,0:T(8,128)} async-done(((f32[512,128]{1,0:T(8,128)}), f32[2048,128]{1,0:T(8,128)}) %all-gather.5.cloned.1.call-update) | async-done | bytes 1048592 | tf_op jit(solution)/shard_map/while/body/eval_jaxpr/all_gather | solution.py:74
  678.9 130.9 %while.44 = (s32[]{:T(128)}, f32[2048,128]{1,0:T(8,128)S(1)}, f32[2048,128]{1,0:T(8,128)}, f32[2048,128]{1,0:T(8,128)}, f32[2048,2048]{1,0:T(8,128)}, /*index=5*...) while((s32[]{:T(128)}, f32[2048,128]{1,0:T(8,128)S(1)}, ...), condition=%wide.region_8.8_spmd, body=%wide.region_7.7_spmd.sunk | while | flops 503365632 | bytes 3017907 | solution.py:43
  811.2 56.2 %all-reduce.13.cloned.1.call-done = f32[2048,128]{1,0:T(8,128)} async-done(((f32[2048,128]{1,0:T(8,128)}), f32[2048,128]{1,0:T(8,128)}) %all-reduce.13.cloned.1.call-update) | async-done | bytes 1048592 | tf_op jit(solution)/shard_map/while/body/eval_jaxpr/psum | solution.py:15
  877.0 29.1 %all-gather.5.cloned.1.call-done = f32[2048,128]{1,0:T(8,128)} async-done(((f32[512,128]{1,0:T(8,128)}), f32[2048,128]{1,0:T(8,128)}) %all-gather.5.cloned.1.call-update) | async-done | bytes 1048592 | tf_op jit(solution)/shard_map/while/body/eval_jaxpr/all_gather | solution.py:74
  906.2 130.9 %while.44 = (s32[]{:T(128)}, f32[2048,128]{1,0:T(8,128)S(1)}, f32[2048,128]{1,0:T(8,128)}, f32[2048,128]{1,0:T(8,128)}, f32[2048,2048]{1,0:T(8,128)}, /*index=5*...) while((s32[]{:T(128)}, f32[2048,128]{1,0:T(8,128)S(1)}, ...), condition=%wide.region_8.8_spmd, body=%wide.region_7.7_spmd.sunk | while | flops 503365632 | bytes 3017907 | solution.py:43
  1038.5 56.2 %all-reduce.13.cloned.1.call-done = f32[2048,128]{1,0:T(8,128)} async-done(((f32[2048,128]{1,0:T(8,128)}), f32[2048,128]{1,0:T(8,128)}) %all-reduce.13.cloned.1.call-update) | async-done | bytes 1048592 | tf_op jit(solution)/shard_map/while/body/eval_jaxpr/psum | solution.py:15
  1104.2 29.1 %all-gather.5.cloned.1.call-done = f32[2048,128]{1,0:T(8,128)} async-done(((f32[512,128]{1,0:T(8,128)}), f32[2048,128]{1,0:T(8,128)}) %all-gather.5.cloned.1.call-update) | async-done | bytes 1048592 | tf_op jit(solution)/shard_map/while/body/eval_jaxpr/all_gather | solution.py:74
  1133.4 130.9 %while.44 = (s32[]{:T(128)}, f32[2048,128]{1,0:T(8,128)S(1)}, f32[2048,128]{1,0:T(8,128)}, f32[2048,128]{1,0:T(8,128)}, f32[2048,2048]{1,0:T(8,128)}, /*index=5*...) while((s32[]{:T(128)}, f32[2048,128]{1,0:T(8,128)S(1)}, ...), condition=%wide.region_8.8_spmd, body=%wide.region_7.7_spmd.sunk | while | flops 503365632 | bytes 3017907 | solution.py:43
  1265.7 56.2 %all-reduce.13.cloned.1.call-done = f32[2048,128]{1,0:T(8,128)} async-done(((f32[2048,128]{1,0:T(8,128)}), f32[2048,128]{1,0:T(8,128)}) %all-reduce.13.cloned.1.call-update) | async-done | bytes 1048592 | tf_op jit(solution)/shard_map/while/body/eval_jaxpr/psum | solution.py:15
  1331.5 29.1 %all-gather.5.cloned.1.call-done = f32[2048,128]{1,0:T(8,128)} async-done(((f32[512,128]{1,0:T(8,128)}), f32[2048,128]{1,0:T(8,128)}) %all-gather.5.cloned.1.call-update) | async-done | bytes 1048592 | tf_op jit(solution)/shard_map/while/body/eval_jaxpr/all_gather | solution.py:74
  1360.7 130.9 %while.44 = (s32[]{:T(128)}, f32[2048,128]{1,0:T(8,128)S(1)}, f32[2048,128]{1,0:T(8,128)}, f32[2048,128]{1,0:T(8,128)}, f32[2048,2048]{1,0:T(8,128)}, /*index=5*...) while((s32[]{:T(128)}, f32[2048,128]{1,0:T(8,128)S(1)}, ...), condition=%wide.region_8.8_spmd, body=%wide.region_7.7_spmd.sunk | while | flops 503365632 | bytes 3017907 | solution.py:43
  1493.0 56.2 %all-reduce.13.cloned.1.call-done = f32[2048,128]{1,0:T(8,128)} async-done(((f32[2048,128]{1,0:T(8,128)}), f32[2048,128]{1,0:T(8,128)}) %all-reduce.13.cloned.1.call-update) | async-done | bytes 1048592 | tf_op jit(solution)/shard_map/while/body/eval_jaxpr/psum | solution.py:15
  1558.8 29.1 %all-gather.5.cloned.1.call-done = f32[2048,128]{1,0:T(8,128)} async-done(((f32[512,128]{1,0:T(8,128)}), f32[2048,128]{1,0:T(8,128)}) %all-gather.5.cloned.1.call-update) | async-done | bytes 1048592 | tf_op jit(solution)/shard_map/while/body/eval_jaxpr/all_gather | solution.py:74
  1588.0 130.9 %while.44 = (s32[]{:T(128)}, f32[2048,128]{1,0:T(8,128)S(1)}, f32[2048,128]{1,0:T(8,128)}, f32[2048,128]{1,0:T(8,128)}, f32[2048,2048]{1,0:T(8,128)}, /*index=5*...) while((s32[]{:T(128)}, f32[2048,128]{1,0:T(8,128)S(1)}, ...), condition=%wide.region_8.8_spmd, body=%wide.region_7.7_spmd.sunk | while | flops 503365632 | bytes 3017907 | solution.py:43
  1720.2 56.2 %all-reduce.13.cloned.1.call-done = f32[2048,128]{1,0:T(8,128)} async-done(((f32[2048,128]{1,0:T(8,128)}), f32[2048,128]{1,0:T(8,128)}) %all-reduce.13.cloned.1.call-update) | async-done | bytes 1048592 | tf_op jit(solution)/shard_map/while/body/eval_jaxpr/psum | solution.py:15
  1786.0 29.1 %all-gather.5.cloned.1.call-done = f32[2048,128]{1,0:T(8,128)} async-done(((f32[512,128]{1,0:T(8,128)}), f32[2048,128]{1,0:T(8,128)}) %all-gather.5.cloned.1.call-update) | async-done | bytes 1048592 | tf_op jit(solution)/shard_map/while/body/eval_jaxpr/all_gather | solution.py:74
  1815.2 130.9 %while.44 = (s32[]{:T(128)}, f32[2048,128]{1,0:T(8,128)S(1)}, f32[2048,128]{1,0:T(8,128)}, f32[2048,128]{1,0:T(8,128)}, f32[2048,2048]{1,0:T(8,128)}, /*index=5*...) while((s32[]{:T(128)}, f32[2048,128]{1,0:T(8,128)S(1)}, ...), condition=%wide.region_8.8_spmd, body=%wide.region_7.7_spmd.sunk | while | flops 503365632 | bytes 3017907 | solution.py:43
  1947.5 56.2 %all-reduce.13.cloned.1.call-done = f32[2048,128]{1,0:T(8,128)} async-done(((f32[2048,128]{1,0:T(8,128)}), f32[2048,128]{1,0:T(8,128)}) %all-reduce.13.cloned.1.call-update) | async-done | bytes 1048592 | tf_op jit(solution)/shard_map/while/body/eval_jaxpr/psum | solution.py:15
  2013.3 29.1 %all-gather.5.cloned.1.call-done = f32[2048,128]{1,0:T(8,128)} async-done(((f32[512,128]{1,0:T(8,128)}), f32[2048,128]{1,0:T(8,128)}) %all-gather.5.cloned.1.call-update) | async-done | bytes 1048592 | tf_op jit(solution)/shard_map/while/body/eval_jaxpr/all_gather | solution.py:74
  2042.5 130.9 %while.44 = (s32[]{:T(128)}, f32[2048,128]{1,0:T(8,128)S(1)}, f32[2048,128]{1,0:T(8,128)}, f32[2048,128]{1,0:T(8,128)}, f32[2048,2048]{1,0:T(8,128)}, /*index=5*...) while((s32[]{:T(128)}, f32[2048,128]{1,0:T(8,128)S(1)}, ...), condition=%wide.region_8.8_spmd, body=%wide.region_7.7_spmd.sunk | while | flops 503365632 | bytes 3017907 | solution.py:43
  2174.7 56.2 %all-reduce.13.cloned.1.call-done = f32[2048,128]{1,0:T(8,128)} async-done(((f32[2048,128]{1,0:T(8,128)}), f32[2048,128]{1,0:T(8,128)}) %all-reduce.13.cloned.1.call-update) | async-done | bytes 1048592 | tf_op jit(solution)/shard_map/while/body/eval_jaxpr/psum | solution.py:15
  2240.5 39.4 %psum.58 = f32[64,128]{1,0:T(8,128)S(1)} all-reduce(f32[64,128]{1,0:T(8,128)S(1)} %fusion.19), channel_id=1, replica_groups=mesh['row'=8,'col'=4] {'row','col'}, use_global_device_ids=true, to_apply=%region_11.12 | all-reduce | flops 8192 | bytes 65536 | tf_op jit(solution)/shard_map/psum | solution.py:94
  (886 shorter events, 1185.6 us)
Async XLA Ops:
  7.2 189.2 %copy-start = (bf16[4096,64]{0,1:T(8,128)(2,1)S(1)}, bf16[4096,64]{0,1:T(8,128)(2,1)}, u32[]{:S(2)}) copy-start(bf16[4096,64]{0,1:T(8,128)(2,1)} %param.15) | copy-start | bytes 1572868
  7.2 64.0 %all-reduce.7.cloned.1.call-start = ((), (), s32[]{:S(2)}) async-start(), calls=%async_computation.1 | async-start | bytes 2097152 | tf_op jit(solution)/shard_map/psum | solution.py:15
  9.6 102.4 %all-reduce.9.cloned.1.call-start = ((), (), s32[]{:S(2)}) async-start(), calls=%async_computation.2 | async-start | bytes 1048576 | tf_op jit(solution)/shard_map/psum | solution.py:15
  73.1 143.6 %reduce-scatter.2.cloned.1.call-start = ((), (), s32[]{:S(2)}) async-start(), calls=%async_computation.3 | async-start | bytes 1310720 | tf_op jit(solution)/shard_map/reduce_scatter | solution.py:70
  190.8 175.6 %all-gather.3.cloned.1.call-start = ((), (), s32[]{:S(2)}) async-start(), calls=%async_computation.4 | async-start | bytes 10485760 | tf_op jit(solution)/shard_map/all_gather | solution.py:53
  194.6 226.6 %all-reduce.11.cloned.1.call-start = ((), (), s32[]{:S(2)}) async-start(), calls=%async_computation.5 | async-start | bytes 131072 | tf_op jit(solution)/shard_map/psum | solution.py:15
  421.3 30.0 %all-gather.5.cloned.1.call-start = ((), (), s32[]{:S(2)}) async-start(), calls=%async_computation.6 | async-start | bytes 1310720 | tf_op jit(solution)/shard_map/while/body/eval_jaxpr/all_gather | solution.py:74
  422.0 217.9 %copy-start.4 = (f32[512,128]{1,0:T(8,128)S(1)}, f32[512,128]{1,0:T(8,128)}, u32[]{:S(2)}) copy-start(f32[512,128]{1,0:T(8,128)} %copy-done.3) | copy-start | bytes 786436 | tf_op jit(solution)/shard_map/while
  422.0 217.9 %all-reduce.13.cloned.1.call-start = ((), (), s32[]{:S(2)}) async-start(), calls=%async_computation.7 | async-start | bytes 2097152 | tf_op jit(solution)/shard_map/while/body/eval_jaxpr/psum | solution.py:15
  648.6 30.2 %all-gather.5.cloned.1.call-start = ((), (), s32[]{:S(2)}) async-start(), calls=%async_computation.6 | async-start | bytes 1310720 | tf_op jit(solution)/shard_map/while/body/eval_jaxpr/all_gather | solution.py:74
  649.4 218.0 %copy-start.4 = (f32[512,128]{1,0:T(8,128)S(1)}, f32[512,128]{1,0:T(8,128)}, u32[]{:S(2)}) copy-start(f32[512,128]{1,0:T(8,128)} %copy-done.3) | copy-start | bytes 786436 | tf_op jit(solution)/shard_map/while
  649.4 218.0 %all-reduce.13.cloned.1.call-start = ((), (), s32[]{:S(2)}) async-start(), calls=%async_computation.7 | async-start | bytes 2097152 | tf_op jit(solution)/shard_map/while/body/eval_jaxpr/psum | solution.py:15
  876.2 29.9 %all-gather.5.cloned.1.call-start = ((), (), s32[]{:S(2)}) async-start(), calls=%async_computation.6 | async-start | bytes 1310720 | tf_op jit(solution)/shard_map/while/body/eval_jaxpr/all_gather | solution.py:74
  876.9 217.8 %copy-start.4 = (f32[512,128]{1,0:T(8,128)S(1)}, f32[512,128]{1,0:T(8,128)}, u32[]{:S(2)}) copy-start(f32[512,128]{1,0:T(8,128)} %copy-done.3) | copy-start | bytes 786436 | tf_op jit(solution)/shard_map/while
  876.9 217.7 %all-reduce.13.cloned.1.call-start = ((), (), s32[]{:S(2)}) async-start(), calls=%async_computation.7 | async-start | bytes 2097152 | tf_op jit(solution)/shard_map/while/body/eval_jaxpr/psum | solution.py:15
  1103.5 29.9 %all-gather.5.cloned.1.call-start = ((), (), s32[]{:S(2)}) async-start(), calls=%async_computation.6 | async-start | bytes 1310720 | tf_op jit(solution)/shard_map/while/body/eval_jaxpr/all_gather | solution.py:74
  1104.2 217.8 %copy-start.4 = (f32[512,128]{1,0:T(8,128)S(1)}, f32[512,128]{1,0:T(8,128)}, u32[]{:S(2)}) copy-start(f32[512,128]{1,0:T(8,128)} %copy-done.3) | copy-start | bytes 786436 | tf_op jit(solution)/shard_map/while
  1104.2 217.7 %all-reduce.13.cloned.1.call-start = ((), (), s32[]{:S(2)}) async-start(), calls=%async_computation.7 | async-start | bytes 2097152 | tf_op jit(solution)/shard_map/while/body/eval_jaxpr/psum | solution.py:15
  1330.7 29.9 %all-gather.5.cloned.1.call-start = ((), (), s32[]{:S(2)}) async-start(), calls=%async_computation.6 | async-start | bytes 1310720 | tf_op jit(solution)/shard_map/while/body/eval_jaxpr/all_gather | solution.py:74
  1331.4 217.8 %copy-start.4 = (f32[512,128]{1,0:T(8,128)S(1)}, f32[512,128]{1,0:T(8,128)}, u32[]{:S(2)}) copy-start(f32[512,128]{1,0:T(8,128)} %copy-done.3) | copy-start | bytes 786436 | tf_op jit(solution)/shard_map/while
  1331.4 217.7 %all-reduce.13.cloned.1.call-start = ((), (), s32[]{:S(2)}) async-start(), calls=%async_computation.7 | async-start | bytes 2097152 | tf_op jit(solution)/shard_map/while/body/eval_jaxpr/psum | solution.py:15
  1558.0 29.9 %all-gather.5.cloned.1.call-start = ((), (), s32[]{:S(2)}) async-start(), calls=%async_computation.6 | async-start | bytes 1310720 | tf_op jit(solution)/shard_map/while/body/eval_jaxpr/all_gather | solution.py:74
  1558.7 217.8 %copy-start.4 = (f32[512,128]{1,0:T(8,128)S(1)}, f32[512,128]{1,0:T(8,128)}, u32[]{:S(2)}) copy-start(f32[512,128]{1,0:T(8,128)} %copy-done.3) | copy-start | bytes 786436 | tf_op jit(solution)/shard_map/while
  1558.7 217.7 %all-reduce.13.cloned.1.call-start = ((), (), s32[]{:S(2)}) async-start(), calls=%async_computation.7 | async-start | bytes 2097152 | tf_op jit(solution)/shard_map/while/body/eval_jaxpr/psum | solution.py:15
  1785.2 29.9 %all-gather.5.cloned.1.call-start = ((), (), s32[]{:S(2)}) async-start(), calls=%async_computation.6 | async-start | bytes 1310720 | tf_op jit(solution)/shard_map/while/body/eval_jaxpr/all_gather | solution.py:74
  1785.9 217.8 %copy-start.4 = (f32[512,128]{1,0:T(8,128)S(1)}, f32[512,128]{1,0:T(8,128)}, u32[]{:S(2)}) copy-start(f32[512,128]{1,0:T(8,128)} %copy-done.3) | copy-start | bytes 786436 | tf_op jit(solution)/shard_map/while
  1786.0 217.7 %all-reduce.13.cloned.1.call-start = ((), (), s32[]{:S(2)}) async-start(), calls=%async_computation.7 | async-start | bytes 2097152 | tf_op jit(solution)/shard_map/while/body/eval_jaxpr/psum | solution.py:15
  2012.5 29.9 %all-gather.5.cloned.1.call-start = ((), (), s32[]{:S(2)}) async-start(), calls=%async_computation.6 | async-start | bytes 1310720 | tf_op jit(solution)/shard_map/while/body/eval_jaxpr/all_gather | solution.py:74
  2013.2 217.8 %copy-start.4 = (f32[512,128]{1,0:T(8,128)S(1)}, f32[512,128]{1,0:T(8,128)}, u32[]{:S(2)}) copy-start(f32[512,128]{1,0:T(8,128)} %copy-done.3) | copy-start | bytes 786436 | tf_op jit(solution)/shard_map/while
  2013.2 217.7 %all-reduce.13.cloned.1.call-start = ((), (), s32[]{:S(2)}) async-start(), calls=%async_computation.7 | async-start | bytes 2097152 | tf_op jit(solution)/shard_map/while/body/eval_jaxpr/psum | solution.py:15
  2239.7 43.5 %copy-start.2 = (f32[2048,128]{1,0:T(8,128)}, f32[2048,128]{1,0:T(8,128)S(1)}, u32[]{:S(2)}) copy-start(f32[2048,128]{1,0:T(8,128)S(1)} %get-tuple-element.328) | copy-start | bytes 3145732
  2239.7 43.5 %copy-start.1 = (bf16[4096,64]{0,1:T(8,128)(2,1)S(1)}, bf16[4096,64]{0,1:T(8,128)(2,1)}, u32[]{:S(2)}) copy-start(bf16[4096,64]{0,1:T(8,128)(2,1)} %param.15) | copy-start | bytes 1572868
  (8 other events, 5.6 us)
Sparse Core Ops, SparseCore 0:
  11.7 59.4 all-reduce.6
  74.1 37.8 all-reduce.8
  190.9 25.8 reduce-scatter.1
  218.2 148.1 all-gather.2
  369.8 51.3 all-reduce.10
  423.9 27.3 all-gather.4
  583.8 56.0 all-reduce.12
  651.6 27.2 all-gather.4
  811.3 56.0 all-reduce.12
  878.9 27.2 all-gather.4
  1038.6 56.0 all-reduce.12
  1106.1 27.2 all-gather.4
  1265.8 56.0 all-reduce.12
  1333.3 27.2 all-gather.4
  1493.1 56.0 all-reduce.12
  1560.6 27.2 all-gather.4
  1720.3 56.0 all-reduce.12
  1787.9 27.2 all-gather.4
  1947.6 56.0 all-reduce.12
  2015.1 27.2 all-gather.4
  2174.8 56.0 all-reduce.12
where the time goes:
time: 2320 us; the launch traced here: 2290 us
  matrix products  1050 us (45%)
  waiting for transfers between devices  987 us (43%)
  local copies, waits for them, and re-layouts  108 us (5%)
  blocking collectives  97 us (4%)
  other arithmetic  29.4 us (1%)
    psum x11, waiting for transfers between devices, spread(): return lax.psum(jnp.where(mine, x, jnp.zeros_like(x)), axis)  593 us
    dot_general x128, matrix products, step(): lax.dot_general(column, solved, (((0,), (0,)), ((), ())), precision=HIGH,...  390 us
    all_gather x8, waiting for transfers between devices, section(): gathered = lax.all_gather(residual, 'col', axis=0, tiled=True)  233 us
    all_gather x1, waiting for transfers between devices, on_device(): lax.all_gather(panel_rows.astype(jnp.bfloat16), 'col', axis=1, tiled=True)  148 us
    dot_general x128, matrix products, tile_solve(): jnp.dot(basis_left.T, right, precision=HIGH)  144 us
    dot_general x128, matrix products, tile_solve(): jnp.dot(jnp.dot(basis_left, scaled, precision=HIGH), basis_right.T, preci...  142 us
    dot_general x128, matrix products, tile_solve(): jnp.dot(basis_left, scaled, precision=HIGH)  134 us
    dot_general x128, matrix products, tile_solve(): jnp.dot(jnp.dot(basis_left.T, right, precision=HIGH), basis_right, precis...  133 us
  transfers between devices with their start and end apart: 21, of which 21 were waited for; matrix products, arithmetic and copies ran while one was open for 1% of the time, Pallas kernels for 0%

commit v1 on v0

v1 whole, which is shorter than its diff:
```python
import functools

import jax
import jax.numpy as jnp
from jax import lax
from jax.experimental import pallas as pl
from jax.experimental.pallas import tpu as pltpu
from jax.sharding import PartitionSpec as P

TILE = 128
W_COLS = 128


HIGH = lax.Precision.HIGHEST


def spread(x, axis, root):
    mine = lax.axis_index(axis) == root
    return lax.psum(jnp.where(mine, x, jnp.zeros_like(x)), axis)


def solve_kernel(groups, where_ref, panel_ref, turn_ref, basis_ref, scale_ref, *refs):
    pieces = refs[:groups]
    out_ref, rounded_ref, right, solved = refs[groups:]
    mine = where_ref[0]
    tiles = pieces[0].shape[0] // TILE
    count = out_ref.shape[0] // TILE
    for distance in range(groups):
        base = lax.rem(mine - distance + groups, groups) * tiles
        for tile in range(tiles):
            start = pl.multiple_of((base + tile) * TILE, TILE)
            right[pl.ds(start, TILE), :] = jnp.dot(
                turn_ref[base + tile],
                pieces[distance][tile * TILE : (tile + 1) * TILE, :],
                precision=HIGH,
                preferred_element_type=jnp.float32,
            )
    solved[...] = jnp.zeros_like(solved)

    def step(index, carry):
        start = pl.multiple_of(index * TILE, TILE)
        rows = pl.ds(start, TILE)
        both = jnp.dot(panel_ref[rows, :], solved[...], preferred_element_type=jnp.float32)
        value = right[rows, :] - (both[:, :W_COLS] + both[:, W_COLS:])
        value = value * scale_ref[rows, :]
        high = value.astype(jnp.bfloat16)
        low = (value - high.astype(jnp.float32)).astype(jnp.bfloat16)
        solved[rows, :W_COLS] = high
        solved[rows, W_COLS:] = low
        right[rows, :] = value
        return carry

    lax.fori_loop(0, count, step, 0)
    for tile in range(count):
        rows = slice(tile * TILE, (tile + 1) * TILE)
        back = jnp.dot(
            basis_ref[tile], right[rows, :], precision=HIGH, preferred_element_type=jnp.float32
        )
        out_ref[rows, :] = back
        rounded_ref[rows, :] = back.astype(jnp.bfloat16)


def solve_rows(where, panel, turn, basis, scale, pieces):
    span = panel.shape[0]
    vmem = pl.BlockSpec(memory_space=pltpu.VMEM)
    groups = len(pieces)
    return pl.pallas_call(
        functools.partial(solve_kernel, groups),
        out_shape=(
            jax.ShapeDtypeStruct((span, W_COLS), jnp.float32),
            jax.ShapeDtypeStruct((span, W_COLS), jnp.bfloat16),
        ),
        in_specs=[pl.BlockSpec(memory_space=pltpu.SMEM)] + [vmem] * (4 + groups),
        out_specs=(vmem, vmem),
        scratch_shapes=[
            pltpu.VMEM((span, W_COLS), jnp.float32),
            pltpu.VMEM((span, 2 * W_COLS), jnp.bfloat16),
        ],
        compiler_params=pltpu.CompilerParams(vmem_limit_bytes=32 * 1024 * 1024),
        cost_estimate=pl.CostEstimate(
            flops=4 * span * span * W_COLS, bytes_accessed=32 * span * TILE * 16, transcendentals=0
        ),
    )(where, panel, turn, basis, scale, *pieces)


def on_device(schur, basis, eigen, schur_basis, rhs, inputs):
    span = schur_basis.shape[1]
    width = schur.shape[1]
    chain = lax.axis_size("row")
    groups = lax.axis_size("col")
    ratio = chain // groups
    row_index = lax.axis_index("row")
    col_index = lax.axis_index("col")
    vectors = basis.reshape(span // TILE, TILE, TILE)
    turn = vectors.transpose(0, 2, 1)

    corner = spread(jnp.concatenate([basis[:W_COLS], eigen[None, :W_COLS]], 0), "row", 0)
    corner_basis, corner_eig = corner[:W_COLS], corner[W_COLS]

    panel_rows = lax.dynamic_slice_in_dim(schur, row_index * span, span, 0)
    own = lax.dynamic_slice_in_dim(vectors, col_index * (width // TILE), width // TILE, 0)
    blocks = panel_rows.reshape(span // TILE, TILE, width)
    left = jnp.einsum("tik,tic->tkc", vectors, blocks, precision=lax.Precision.HIGH)
    left = left.reshape(span, width // TILE, TILE)
    rotated = jnp.einsum("rtj,tjl->tlr", left, own, precision=lax.Precision.HIGH)
    panel = lax.all_gather(
        rotated.reshape(width, span).astype(jnp.bfloat16), "col", axis=0, tiled=True
    )
    scale = 1.0 / (eigen[:, None] + corner_eig[None, :])

    window = spread(schur_basis[:, :W_COLS], "row", 0)
    offset = row_index % ratio * span
    mine = lax.dynamic_slice_in_dim(window, offset, span, 0)
    own_window = spread(mine, "col", row_index // ratio)
    partial_value = jnp.dot(rhs, own_window, preferred_element_type=jnp.float32)
    projected = lax.psum(partial_value, "row").astype(jnp.bfloat16)
    coords = lax.dot_general(
        schur_basis, projected, (((0,), (0,)), ((), ())), preferred_element_type=jnp.float32
    )
    share = lax.psum_scatter(coords, "col", scatter_dimension=0, tiled=True)
    residual = -jnp.dot(share, corner_basis, precision=HIGH)
    where = col_index.astype(jnp.int32)[None]
    mapped = lax.dot_general(
        inputs, schur_basis, (((0,), (0,)), ((), ())), preferred_element_type=jnp.float32
    )

    def update(index, block):
        return lax.dot_general(
            schur[index * span : (index + 1) * span],
            block.astype(jnp.float32),
            (((0,), (0,)), ((), ())),
            precision=lax.Precision.HIGH,
            preferred_element_type=jnp.float32,
        )

    solution = jnp.zeros((span, W_COLS), jnp.float32)
    for index in range(chain):
        pieces = [residual] + [
            lax.ppermute(residual, "col", [(g, (g + d) % groups) for g in range(groups)])
            for d in range(1, groups)
        ]
        solved, rounded = solve_rows(where, panel, turn, vectors, scale, pieces)
        solution = jnp.where(row_index == index, solved, solution)
        if index + 1 < chain:
            block = lax.ppermute(rounded, "row", [(index, index + 1)])
            near = update(index, block)
        if index > 0 and index + 1 < chain:
            residual = residual - far
        if index + 1 < chain:
            residual = residual - near
        if index + 2 < chain:
            blocks = [lax.ppermute(rounded, "row", [(index, r)]) for r in range(index + 2, chain)]
            far = update(index, functools.reduce(jnp.add, blocks))
        else:
            far = jnp.zeros_like(residual)
    solution = jnp.dot(solution, corner_basis.T, precision=HIGH)
    gain = lax.psum(jnp.dot(mapped, solution, precision=HIGH), ("row", "col"))
    feedback = jnp.dot(gain, window.astype(jnp.float32).T, precision=HIGH)
    return (solution, feedback)


def solution(mesh):
    placed = (
        P(None, ("row", "col")),
        P("row", None),
        P("row"),
        P("col", "row"),
        P("col", "row"),
        P("col", None),
    )
    return jax.shard_map(
        on_device,
        mesh=mesh,
        in_specs=placed,
        out_specs=(P("row", None), P(None, "col")),
        check_vma=False,
    )
```

time: 2320 us -> 803 us (0.35)
  matrix products: 1050 us -> 105 us
  waiting for transfers between devices: 987 us -> 359 us
  starting transfers between devices: 0.99 us -> 87.3 us
  local copies, waits for them, and re-layouts: 108 us -> 24.1 us
  Pallas kernels: 0 us -> 59.9 us
  blocking collectives: 97 us -> 140 us
    dot_general x648 -> x17, matrix products: 1010 us -> 70.9 us  [the longest x13 59.3 us: update(): lax.dot_general(schur[index * span:(index + 1) * span], block.astype(jnp....]
    psum x11 -> x3, waiting for transfers between devices: 593 us -> 99.6 us  [spread(): return lax.psum(jnp.where(mine, x, jnp.zeros_like(x)), axis)]
    all_gather x9 -> x1, waiting for transfers between devices: 382 us -> 128 us  [on_device(): lax.all_gather(rotated.reshape(width, span).astype(jnp.bfloat16), 'col',...]
    ppermute x0 -> x52, waiting for transfers between devices: none -> 128 us  [the longest x24 115 us: on_device(): lax.ppermute(residual, 'col', [(g, (g + d) % groups) for g in range(group...]
    dynamic_slice x128 -> x1, local copies, waits for them, and re-layouts: 98 us -> 2.72 us  [on_device(): panel_rows = lax.dynamic_slice_in_dim(schur, row_index * span, span, 0)]
    ppermute x0 -> x52, starting transfers between devices: none -> 86.9 us  [the longest x24 61.9 us: on_device(): lax.ppermute(residual, 'col', [(g, (g + d) % groups) for g in range(group...]
    pallas_call x0 -> x8, Pallas kernels: none -> 59.9 us  [solve_rows(): pl.pallas_call(functools.partial(solve_kernel, groups), out_shape=(jax.Sh...]
    psum x1, blocking collectives: 39.4 us -> 82.1 us  [on_device(): gain = lax.psum(jnp.dot(mapped, solution, precision=HIGH), ('row', 'col'))]
  transfers between devices with their start and end apart: 21 -> 57, of which waited for: 21 -> 23; matrix products, arithmetic and copies ran while one was open for 1% -> 11% of each run, Pallas kernels for 0% -> 1%
where the time goes in v1:
time: 803 us; the launch traced here: 796 us
  waiting for transfers between devices  359 us (45%)
  blocking collectives  140 us (17%)
  matrix products  105 us (13%)
  starting transfers between devices  87.3 us (11%)
  Pallas kernels  59.9 us (7%)
  local copies, waits for them, and re-layouts  24.1 us (3%)
  between operations  15 us (2%)
    all_gather x1, waiting for transfers between devices, on_device(): lax.all_gather(rotated.reshape(width, span).astype(jnp.bfloat16), 'col',...  128 us
    ppermute x24, waiting for transfers between devices, on_device(): lax.ppermute(residual, 'col', [(g, (g + d) % groups) for g in range(group...  115 us
    psum x3, waiting for transfers between devices, spread(): return lax.psum(jnp.where(mine, x, jnp.zeros_like(x)), axis)  99.6 us
    psum x1, blocking collectives, on_device(): gain = lax.psum(jnp.dot(mapped, solution, precision=HIGH), ('row', 'col'))  82.1 us
    ppermute x24, starting transfers between devices, on_device(): lax.ppermute(residual, 'col', [(g, (g + d) % groups) for g in range(group...  61.9 us
    pallas_call x8, Pallas kernels, solve_rows(): pl.pallas_call(functools.partial(solve_kernel, groups), out_shape=(jax.Sh...  59.9 us
    dot_general x13, matrix products, update(): lax.dot_general(schur[index * span:(index + 1) * span], block.astype(jnp....  59.3 us
    psum x1, blocking collectives, on_device(): projected = lax.psum(partial_value, 'row').astype(jnp.bfloat16)  57.7 us
  transfers between devices with their start and end apart: 57, of which 23 were waited for; matrix products, arithmetic and copies ran while one was open for 11% of the time, Pallas kernels for 1%

profile of v1, /device:TPU:0, one launch (start us, length us, event | category | flops | bytes accessed | tf_op | source)
XLA Modules:
  0.0 796.2 jit_solution(3325720963344094723)
XLA Ops:
  9.7 61.5 %all-reduce.7.cloned.1.call-done = bf16[4096,128]{1,0:T(8,128)(2,1)} async-done(((bf16[4096,128]{1,0:T(8,128)(2,1)}), bf16[4096,128]{1,0:T(8,128)(2,1)}) %all-reduce.7.cloned.1.call-update) | async-done | bytes 1048592 | tf_op jit(solution)/shard_map/psum | solution.py:19
  73.9 38.1 %all-reduce.9.cloned.1.call-done = bf16[2048,128]{1,0:T(8,128)(2,1)} async-done(((bf16[2048,128]{1,0:T(8,128)(2,1)}), bf16[2048,128]{1,0:T(8,128)(2,1)}) %all-reduce.9.cloned.1.call-update) | async-done | bytes 524304 | tf_op jit(solution)/shard_map/psum | solution.py:19
  112.0 11.7 %convolution_bitcast_fusion = f32[4096,128]{0,1:T(8,128)S(1)} fusion(bf16[2048,128]{1,0:T(8,128)(2,1)} %all-reduce.9.cloned.1.call-done, bf16[4096,2048]{1,0:T(8,128)(2,1)} %param.10), kind=kOutput, calls=%fused_computation | convolution fusion | flops 2147483648 | bytes 19398656 | tf_op jit(solution)/shard_map/dot_general | solution.py:115
  123.7 57.7 %all-reduce.10 = bf16[4096,128]{0,1:T(8,128)(2,1)} all-reduce(f32[4096,128]{0,1:T(8,128)S(1)} %convolution_bitcast_fusion), channel_id=1, replica_groups=mesh['row'=8,'col'=4] {'row'}, use_global_device_ids=true, to_apply=%region_3.4 | all-reduce | flops 524288 | bytes 3145728 | tf_op jit(solution)/shard_map/psum | solution.py:116
  181.4 9.4 %convolution_bitcast_fusion.1 = f32[2048,128]{0,1:T(8,128)} fusion(bf16[4096,2048]{1,0:T(8,128)(2,1)} %param.9, bf16[4096,128]{0,1:T(8,128)(2,1)} %all-reduce.10), kind=kOutput, calls=%fused_computation.28 | convolution fusion | flops 2147483648 | bytes 18874368 | tf_op jit(solution)/shard_map/dot_general | solution.py:117
  224.1 5.7 collective-permute-done.refs_1_
  229.8 21.0 %collective-permute-done.1.refs_2_ = f32[512,128]{1,0:T(8,128)S(1)} collective-permute-done((f32[512,128]{1,0:T(8,128)S(1)}, f32[512,128]{1,0:T(8,128)S(1)}, u32[]{:S(2)}, u32[]{:S(2)}) %collective-permute-start.1) | collective-permute-done | bytes 262176 | tf_op jit(solution)/shard_map/ppermute | solution.py:139
  251.6 128.2 %all-gather.2.cloned.1.call-done.panel_ref = bf16[2048,2048]{1,0:T(8,128)(2,1)} async-done(((bf16[512,2048]{1,0:T(8,128)(2,1)}), bf16[2048,2048]{1,0:T(8,128)(2,1)}) %all-gather.2.cloned.1.call-update) | async-done | bytes 8388624 | tf_op jit(solution)/shard_map/all_gather | solution.py:106
  385.3 7.2 shard_map.77
  405.7 6.0 collective-permute-done.10.refs_1_
  411.7 10.3 %collective-permute-done.11.refs_2_ = f32[512,128]{1,0:T(8,128)S(1)} collective-permute-done((f32[512,128]{1,0:T(8,128)S(1)}, f32[512,128]{1,0:T(8,128)S(1)}, u32[]{:S(2)}, u32[]{:S(2)}) %collective-permute-start.11) | collective-permute-done | bytes 262176 | tf_op jit(solution)/shard_map/ppermute | solution.py:139
  422.0 7.2 shard_map.78
  447.3 5.6 collective-permute-done.9
  457.4 5.7 collective-permute-start.19
  467.5 8.2 %collective-permute-done.20.refs_2_ = f32[512,128]{1,0:T(8,128)S(1)} collective-permute-done((f32[512,128]{1,0:T(8,128)S(1)}, f32[512,128]{1,0:T(8,128)S(1)}, u32[]{:S(2)}, u32[]{:S(2)}) %collective-permute-start.20) | collective-permute-done | bytes 262176 | tf_op jit(solution)/shard_map/ppermute | solution.py:139
  475.7 7.2 shard_map.79
  507.0 6.1 collective-permute-done.28.refs_2_
  513.1 7.2 shard_map.80
  533.1 9.8 %collective-permute-start.34 = (f32[512,128]{1,0:T(8,128)S(1)}, f32[512,128]{1,0:T(8,128)S(1)}, u32[]{:S(2)}, u32[]{:S(2)}) collective-permute-start(f32[512,128]{1,0:T(8,128)S(1)} %fusion.62.refs_0_), channel_id=1, source_target_pairs={{0,1},{1,2},{2,3},{3,0},{4,5},{5,6},{6,7},{7,4},{8,9},{9,10},{10,1... | collective-permute-start | bytes 786440 | tf_op jit(solution)/shard_map/ppermute | solution.py:139
  546.7 14.1 %collective-permute-done.35.refs_2_ = f32[512,128]{1,0:T(8,128)S(1)} collective-permute-done((f32[512,128]{1,0:T(8,128)S(1)}, f32[512,128]{1,0:T(8,128)S(1)}, u32[]{:S(2)}, u32[]{:S(2)}) %collective-permute-start.35) | collective-permute-done | bytes 262176 | tf_op jit(solution)/shard_map/ppermute | solution.py:139
  560.8 7.2 shard_map.81
  580.3 6.2 collective-permute-start.40
  593.2 10.6 %collective-permute-done.41.refs_2_ = f32[512,128]{1,0:T(8,128)S(1)} collective-permute-done((f32[512,128]{1,0:T(8,128)S(1)}, f32[512,128]{1,0:T(8,128)S(1)}, u32[]{:S(2)}, u32[]{:S(2)}) %collective-permute-start.41) | collective-permute-done | bytes 262176 | tf_op jit(solution)/shard_map/ppermute | solution.py:139
  603.8 7.2 shard_map.82
  622.4 6.1 collective-permute-start.45
  631.9 6.3 collective-permute-done.45.refs_1_
  638.2 10.1 %collective-permute-done.46.refs_2_ = f32[512,128]{1,0:T(8,128)S(1)} collective-permute-done((f32[512,128]{1,0:T(8,128)S(1)}, f32[512,128]{1,0:T(8,128)S(1)}, u32[]{:S(2)}, u32[]{:S(2)}) %collective-permute-start.46) | collective-permute-done | bytes 262176 | tf_op jit(solution)/shard_map/ppermute | solution.py:139
  648.3 7.2 shard_map.83
  666.1 6.1 collective-permute-start.49
  674.9 9.6 %fusion.143 = f32[64,2048]{1,0:T(8,128)} fusion(bf16[4096,64]{0,1:T(8,128)(2,1)S(1)} %copy-done, bf16[4096,2048]{1,0:T(8,128)(2,1)} %param.9), kind=kOutput, calls=%fused_computation.103 | convolution fusion | flops 1073741824 | bytes 17825792 | tf_op jit(solution)/shard_map/dot_general | solution.py:123
  694.0 9.2 %shard_map.84 = (f32[2048,128]{1,0:T(8,128)S(1)}, bf16[2048,128]{1,0:T(8,128)(2,1)}) custom-call(s32[1]{0:T(128)} %bitcast.where_ref, bf16[2048,2048]{1,0:T(8,128)(2,1)S(1)} %copy-done.2, f32[16,128,128]{2,1,0:T(8,128)S(1)} %copy.54.turn_ref, f32[16,128,128]{2,1,0:T(8,128)S(1)} %bitcast.102, f32[2048,128]{1,0:T(8,128)S(1)} %copy-done.5, ...), custom_call_target="tpu_custom_call" | custom-call | flops 2147483648 | bytes 134217728 | tf_op jit(solution)/shard_map/pallas_call | solution.py:67
  705.2 82.1 %psum.39 = f32[64,128]{1,0:T(8,128)S(1)} all-reduce(f32[64,128]{1,0:T(8,128)S(1)} %fusion.144), channel_id=1, replica_groups=mesh['row'=8,'col'=4] {'row','col'}, use_global_device_ids=true, to_apply=%region_5.6 | all-reduce | flops 8192 | bytes 65536 | tf_op jit(solution)/shard_map/psum | solution.py:157
  (185 shorter events, 185.1 us)
Async XLA Ops:
  7.2 64.0 %all-reduce.7.cloned.1.call-start = ((), (), s32[]{:S(2)}) async-start(), calls=%async_computation.3 | async-start | bytes 2097152 | tf_op jit(solution)/shard_map/psum | solution.py:19
  9.6 102.4 %all-reduce.9.cloned.1.call-start = ((), (), s32[]{:S(2)}) async-start(), calls=%async_computation.4 | async-start | bytes 1048576 | tf_op jit(solution)/shard_map/psum | solution.py:19
  73.2 139.4 %all-reduce.5.cloned.1.call-start = ((), (), s32[]{:S(2)}) async-start(), calls=%async_computation.2 | async-start | bytes 139264 | tf_op jit(solution)/shard_map/psum | solution.py:19
  73.9 143.3 %reduce-scatter.2.cloned.1.call-start = ((), (), s32[]{:S(2)}) async-start(), calls=%async_computation.5 | async-start | bytes 1310720 | tf_op jit(solution)/shard_map/reduce_scatter | solution.py:120
  190.9 188.9 %all-gather.2.cloned.1.call-start = ((), (), s32[]{:S(2)}) async-start(), calls=%async_computation.1 | async-start | bytes 10485760 | tf_op jit(solution)/shard_map/all_gather | solution.py:106
  218.7 11.1 %collective-permute-start = (f32[512,128]{1,0:T(8,128)S(1)}, f32[512,128]{1,0:T(8,128)S(1)}, u32[]{:S(2)}, u32[]{:S(2)}) collective-permute-start(f32[512,128]{1,0:T(8,128)S(1)} %convolution_negate_fusion.refs_0_), channel_id=1, source_target_pairs={{0,1},{1,2},{2,3},{3,0},{4,5},{5,6},{6,7},{7,4},{8,9},{9,10},{10,1... | collective-permute-start | bytes 786440 | tf_op jit(solution)/shard_map/ppermute | solution.py:139
  218.8 32.1 %collective-permute-start.1 = (f32[512,128]{1,0:T(8,128)S(1)}, f32[512,128]{1,0:T(8,128)S(1)}, u32[]{:S(2)}, u32[]{:S(2)}) collective-permute-start(f32[512,128]{1,0:T(8,128)S(1)} %convolution_negate_fusion.refs_0_), channel_id=1, source_target_pairs={{0,2},{1,3},{2,0},{3,1},{4,6},{5,7},{6,4},{7,5},{8,10},{9,11},{10,... | collective-permute-start | bytes 786440 | tf_op jit(solution)/shard_map/ppermute | solution.py:139
  220.2 30.6 %collective-permute-start.2 = (f32[512,128]{1,0:T(8,128)S(1)}, f32[512,128]{1,0:T(8,128)S(1)}, u32[]{:S(2)}, u32[]{:S(2)}) collective-permute-start(f32[512,128]{1,0:T(8,128)S(1)} %convolution_negate_fusion.refs_0_), channel_id=1, source_target_pairs={{0,3},{1,0},{2,1},{3,2},{4,7},{5,4},{6,5},{7,6},{8,11},{9,8},{10,9... | collective-permute-start | bytes 786440 | tf_op jit(solution)/shard_map/ppermute | solution.py:139
  400.5 11.2 %collective-permute-start.10 = (f32[512,128]{1,0:T(8,128)S(1)}, f32[512,128]{1,0:T(8,128)S(1)}, u32[]{:S(2)}, u32[]{:S(2)}) collective-permute-start(f32[512,128]{1,0:T(8,128)S(1)} %fusion.29.refs_0_), channel_id=1, source_target_pairs={{0,1},{1,2},{2,3},{3,0},{4,5},{5,6},{6,7},{7,4},{8,9},{9,10},{10,1... | collective-permute-start | bytes 786440 | tf_op jit(solution)/shard_map/ppermute | solution.py:139
  400.6 21.4 %collective-permute-start.11 = (f32[512,128]{1,0:T(8,128)S(1)}, f32[512,128]{1,0:T(8,128)S(1)}, u32[]{:S(2)}, u32[]{:S(2)}) collective-permute-start(f32[512,128]{1,0:T(8,128)S(1)} %fusion.29.refs_0_), channel_id=1, source_target_pairs={{0,2},{1,3},{2,0},{3,1},{4,6},{5,7},{6,4},{7,5},{8,10},{9,11},{10,... | collective-permute-start | bytes 786440 | tf_op jit(solution)/shard_map/ppermute | solution.py:139
  402.4 19.6 %collective-permute-start.12 = (f32[512,128]{1,0:T(8,128)S(1)}, f32[512,128]{1,0:T(8,128)S(1)}, u32[]{:S(2)}, u32[]{:S(2)}) collective-permute-start(f32[512,128]{1,0:T(8,128)S(1)} %fusion.29.refs_0_), channel_id=1, source_target_pairs={{0,3},{1,0},{2,1},{3,2},{4,7},{5,4},{6,5},{7,6},{8,11},{9,8},{10,9... | collective-permute-start | bytes 786440 | tf_op jit(solution)/shard_map/ppermute | solution.py:139
  404.4 29.6 %collective-permute-start.4 = (bf16[2048,128]{1,0:T(8,128)(2,1)S(1)}, bf16[2048,128]{1,0:T(8,128)(2,1)S(1)}, u32[]{:S(2)}, u32[]{:S(2)}) collective-permute-start(bf16[2048,128]{1,0:T(8,128)(2,1)S(1)} %get-tuple-element.17), channel_id=1, source_target_pairs={{0,8},{1,9},{2,10},{3,11}} | collective-permute-start | bytes 1572872 | tf_op jit(solution)/shard_map/ppermute | solution.py:152
  430.0 11.6 %collective-permute-start.5 = (bf16[2048,128]{1,0:T(8,128)(2,1)S(1)}, bf16[2048,128]{1,0:T(8,128)(2,1)S(1)}, u32[]{:S(2)}, u32[]{:S(2)}) collective-permute-start(bf16[2048,128]{1,0:T(8,128)(2,1)S(1)} %get-tuple-element.17), channel_id=1, source_target_pairs={{0,12},{1,13},{2,14},{3,15}} | collective-permute-start | bytes 1572872 | tf_op jit(solution)/shard_map/ppermute | solution.py:152
  432.7 12.3 %collective-permute-start.7 = (bf16[2048,128]{1,0:T(8,128)(2,1)S(1)}, bf16[2048,128]{1,0:T(8,128)(2,1)S(1)}, u32[]{:S(2)}, u32[]{:S(2)}) collective-permute-start(bf16[2048,128]{1,0:T(8,128)(2,1)S(1)} %get-tuple-element.17), channel_id=1, source_target_pairs={{0,20},{1,21},{2,22},{3,23}} | collective-permute-start | bytes 1572872 | tf_op jit(solution)/shard_map/ppermute | solution.py:152
  434.0 13.3 %collective-permute-start.8 = (bf16[2048,128]{1,0:T(8,128)(2,1)S(1)}, bf16[2048,128]{1,0:T(8,128)(2,1)S(1)}, u32[]{:S(2)}, u32[]{:S(2)}) collective-permute-start(bf16[2048,128]{1,0:T(8,128)(2,1)S(1)} %get-tuple-element.17), channel_id=1, source_target_pairs={{0,24},{1,25},{2,26},{3,27}} | collective-permute-start | bytes 1572872 | tf_op jit(solution)/shard_map/ppermute | solution.py:152
  435.3 17.5 %collective-permute-start.9 = (bf16[2048,128]{1,0:T(8,128)(2,1)S(1)}, bf16[2048,128]{1,0:T(8,128)(2,1)S(1)}, u32[]{:S(2)}, u32[]{:S(2)}) collective-permute-start(bf16[2048,128]{1,0:T(8,128)(2,1)S(1)} %get-tuple-element.17), channel_id=1, source_target_pairs={{0,28},{1,29},{2,30},{3,31}} | collective-permute-start | bytes 1572872 | tf_op jit(solution)/shard_map/ppermute | solution.py:152
  463.2 12.6 %collective-permute-start.20 = (f32[512,128]{1,0:T(8,128)S(1)}, f32[512,128]{1,0:T(8,128)S(1)}, u32[]{:S(2)}, u32[]{:S(2)}) collective-permute-start(f32[512,128]{1,0:T(8,128)S(1)} %fusion.38.refs_0_), channel_id=1, source_target_pairs={{0,2},{1,3},{2,0},{3,1},{4,6},{5,7},{6,4},{7,5},{8,10},{9,11},{10,... | collective-permute-start | bytes 786440 | tf_op jit(solution)/shard_map/ppermute | solution.py:139
  463.2 12.6 %collective-permute-start.21 = (f32[512,128]{1,0:T(8,128)S(1)}, f32[512,128]{1,0:T(8,128)S(1)}, u32[]{:S(2)}, u32[]{:S(2)}) collective-permute-start(f32[512,128]{1,0:T(8,128)S(1)} %fusion.38.refs_0_), channel_id=1, source_target_pairs={{0,3},{1,0},{2,1},{3,2},{4,7},{5,4},{6,5},{7,6},{8,11},{9,8},{10,9... | collective-permute-start | bytes 786440 | tf_op jit(solution)/shard_map/ppermute | solution.py:139
  496.4 10.6 %collective-permute-start.27 = (f32[512,128]{1,0:T(8,128)S(1)}, f32[512,128]{1,0:T(8,128)S(1)}, u32[]{:S(2)}, u32[]{:S(2)}) collective-permute-start(f32[512,128]{1,0:T(8,128)S(1)} %fusion.50.refs_0_), channel_id=1, source_target_pairs={{0,1},{1,2},{2,3},{3,0},{4,5},{5,6},{6,7},{7,4},{8,9},{9,10},{10,1... | collective-permute-start | bytes 786440 | tf_op jit(solution)/shard_map/ppermute | solution.py:139
  500.0 13.1 %collective-permute-start.28 = (f32[512,128]{1,0:T(8,128)S(1)}, f32[512,128]{1,0:T(8,128)S(1)}, u32[]{:S(2)}, u32[]{:S(2)}) collective-permute-start(f32[512,128]{1,0:T(8,128)S(1)} %fusion.50.refs_0_), channel_id=1, source_target_pairs={{0,2},{1,3},{2,0},{3,1},{4,6},{5,7},{6,4},{7,5},{8,10},{9,11},{10,... | collective-permute-start | bytes 786440 | tf_op jit(solution)/shard_map/ppermute | solution.py:139
  533.1 13.6 %collective-permute-start.34 = (f32[512,128]{1,0:T(8,128)S(1)}, f32[512,128]{1,0:T(8,128)S(1)}, u32[]{:S(2)}, u32[]{:S(2)}) collective-permute-start(f32[512,128]{1,0:T(8,128)S(1)} %fusion.62.refs_0_), channel_id=1, source_target_pairs={{0,1},{1,2},{2,3},{3,0},{4,5},{5,6},{6,7},{7,4},{8,9},{9,10},{10,1... | collective-permute-start | bytes 786440 | tf_op jit(solution)/shard_map/ppermute | solution.py:139
  542.9 18.0 %collective-permute-start.35 = (f32[512,128]{1,0:T(8,128)S(1)}, f32[512,128]{1,0:T(8,128)S(1)}, u32[]{:S(2)}, u32[]{:S(2)}) collective-permute-start(f32[512,128]{1,0:T(8,128)S(1)} %fusion.62.refs_0_), channel_id=1, source_target_pairs={{0,2},{1,3},{2,0},{3,1},{4,6},{5,7},{6,4},{7,5},{8,10},{9,11},{10,... | collective-permute-start | bytes 786440 | tf_op jit(solution)/shard_map/ppermute | solution.py:139
  542.9 18.0 %collective-permute-start.36 = (f32[512,128]{1,0:T(8,128)S(1)}, f32[512,128]{1,0:T(8,128)S(1)}, u32[]{:S(2)}, u32[]{:S(2)}) collective-permute-start(f32[512,128]{1,0:T(8,128)S(1)} %fusion.62.refs_0_), channel_id=1, source_target_pairs={{0,3},{1,0},{2,1},{3,2},{4,7},{5,4},{6,5},{7,6},{8,11},{9,8},{10,9... | collective-permute-start | bytes 786440 | tf_op jit(solution)/shard_map/ppermute | solution.py:139
  580.3 12.9 %collective-permute-start.40 = (f32[512,128]{1,0:T(8,128)S(1)}, f32[512,128]{1,0:T(8,128)S(1)}, u32[]{:S(2)}, u32[]{:S(2)}) collective-permute-start(f32[512,128]{1,0:T(8,128)S(1)} %fusion.74.refs_0_), channel_id=1, source_target_pairs={{0,1},{1,2},{2,3},{3,0},{4,5},{5,6},{6,7},{7,4},{8,9},{9,10},{10,1... | collective-permute-start | bytes 786440 | tf_op jit(solution)/shard_map/ppermute | solution.py:139
  586.5 17.3 %collective-permute-start.41 = (f32[512,128]{1,0:T(8,128)S(1)}, f32[512,128]{1,0:T(8,128)S(1)}, u32[]{:S(2)}, u32[]{:S(2)}) collective-permute-start(f32[512,128]{1,0:T(8,128)S(1)} %fusion.74.refs_0_), channel_id=1, source_target_pairs={{0,2},{1,3},{2,0},{3,1},{4,6},{5,7},{6,4},{7,5},{8,10},{9,11},{10,... | collective-permute-start | bytes 786440 | tf_op jit(solution)/shard_map/ppermute | solution.py:139
  586.5 17.3 %collective-permute-start.42 = (f32[512,128]{1,0:T(8,128)S(1)}, f32[512,128]{1,0:T(8,128)S(1)}, u32[]{:S(2)}, u32[]{:S(2)}) collective-permute-start(f32[512,128]{1,0:T(8,128)S(1)} %fusion.74.refs_0_), channel_id=1, source_target_pairs={{0,3},{1,0},{2,1},{3,2},{4,7},{5,4},{6,5},{7,6},{8,11},{9,8},{10,9... | collective-permute-start | bytes 786440 | tf_op jit(solution)/shard_map/ppermute | solution.py:139
  622.4 15.8 %collective-permute-start.45 = (f32[512,128]{1,0:T(8,128)S(1)}, f32[512,128]{1,0:T(8,128)S(1)}, u32[]{:S(2)}, u32[]{:S(2)}) collective-permute-start(f32[512,128]{1,0:T(8,128)S(1)} %fusion.86.refs_0_), channel_id=1, source_target_pairs={{0,1},{1,2},{2,3},{3,0},{4,5},{5,6},{6,7},{7,4},{8,9},{9,10},{10,1... | collective-permute-start | bytes 786440 | tf_op jit(solution)/shard_map/ppermute | solution.py:139
  628.5 19.8 %collective-permute-start.46 = (f32[512,128]{1,0:T(8,128)S(1)}, f32[512,128]{1,0:T(8,128)S(1)}, u32[]{:S(2)}, u32[]{:S(2)}) collective-permute-start(f32[512,128]{1,0:T(8,128)S(1)} %fusion.86.refs_0_), channel_id=1, source_target_pairs={{0,2},{1,3},{2,0},{3,1},{4,6},{5,7},{6,4},{7,5},{8,10},{9,11},{10,... | collective-permute-start | bytes 786440 | tf_op jit(solution)/shard_map/ppermute | solution.py:139
  631.5 16.8 %collective-permute-start.47 = (f32[512,128]{1,0:T(8,128)S(1)}, f32[512,128]{1,0:T(8,128)S(1)}, u32[]{:S(2)}, u32[]{:S(2)}) collective-permute-start(f32[512,128]{1,0:T(8,128)S(1)} %fusion.86.refs_0_), channel_id=1, source_target_pairs={{0,3},{1,0},{2,1},{3,2},{4,7},{5,4},{6,5},{7,6},{8,11},{9,8},{10,9... | collective-permute-start | bytes 786440 | tf_op jit(solution)/shard_map/ppermute | solution.py:139
  666.1 18.3 %collective-permute-start.49 = (f32[512,128]{1,0:T(8,128)S(1)}, f32[512,128]{1,0:T(8,128)S(1)}, u32[]{:S(2)}, u32[]{:S(2)}) collective-permute-start(f32[512,128]{1,0:T(8,128)S(1)} %fusion.98.refs_0_), channel_id=1, source_target_pairs={{0,1},{1,2},{2,3},{3,0},{4,5},{5,6},{6,7},{7,4},{8,9},{9,10},{10,1... | collective-permute-start | bytes 786440 | tf_op jit(solution)/shard_map/ppermute | solution.py:139
  672.3 17.1 %collective-permute-start.50 = (f32[512,128]{1,0:T(8,128)S(1)}, f32[512,128]{1,0:T(8,128)S(1)}, u32[]{:S(2)}, u32[]{:S(2)}) collective-permute-start(f32[512,128]{1,0:T(8,128)S(1)} %fusion.98.refs_0_), channel_id=1, source_target_pairs={{0,2},{1,3},{2,0},{3,1},{4,6},{5,7},{6,4},{7,5},{8,10},{9,11},{10,... | collective-permute-start | bytes 786440 | tf_op jit(solution)/shard_map/ppermute | solution.py:139
  672.7 16.7 %collective-permute-start.51 = (f32[512,128]{1,0:T(8,128)S(1)}, f32[512,128]{1,0:T(8,128)}, u32[]{:S(2)}, u32[]{:S(2)}) collective-permute-start(f32[512,128]{1,0:T(8,128)S(1)} %fusion.98.refs_0_), channel_id=1, source_target_pairs={{0,3},{1,0},{2,1},{3,2},{4,7},{5,4},{6,5},{7,6},{8,11},{9,8},{10,9... | collective-permute-start | bytes 786440 | tf_op jit(solution)/shard_map/ppermute | solution.py:139
  (53 other events, 1323.1 us)
Sparse Core Ops, SparseCore 0:
  11.7 59.4 all-reduce.6
  74.1 37.8 all-reduce.8
  115.1 49.9 all-reduce.4
  191.0 26.1 reduce-scatter.1
  218.6 161.1 all-gather.1
